TPU v7x, 32 devices: a whole 2x2x4 slice. The times are simulated.
32 devices in a mesh: gx: 8 (over z, x), gy: 4 (over y, core).
Axes of the slice: x: 2, y: 2, z: 4, core: 2. Of those that a mesh axis runs over, the one named last changes fastest.
Arguments:
- pooled: bfloat16 [4096, 8, 128], P(('gx', 'gy')), may hold values from -6 to 6
- cotangent: bfloat16 [4096, 28, 128], P(('gx', 'gy')), may hold values from -0.09375 to 0.09375
- bilinear: bfloat16 [7, 128, 128], replicated, may hold values from -0.5 to 0.5
- bag_ids: int32 [4096, 8, 4], P(('gx', 'gy')), may hold values from 0 to 8191, as said below
- bag_lens: int32 [4096, 8], P(('gx', 'gy')), may hold values from 1 to 4
- row_home: int32 [8, 8192], replicated, may hold values from 0 to 8191, as said below
Outputs:
- weight_grad: float32 [7, 128, 128], replicated
- table_grad: float32 [8192, 8, 128], P(('gx', 'gy'))
Inputs may be any that keep to these rules, and one draw needn't show every extreme that they name: Each row row_home[f] is a permutation; row r of field f's table is stored at position row_home[f, r] of table_grad's first dimension. Only the first bag_lens entries of a bag are live. The stored position q = row_home[f, bag_ids[sample, f, k]] of an entry lies in the block of 256 positions of device q // 256 (devices in gx+gy order); among all entries of one device's samples, live or not, at most 256 lie in any one device's block; in every device's entries some block is hit exactly 256 times, and one block is hit exactly 256 times by the entries of every device.
All inputs are finite; a program needn't handle non-finite values.
Results may differ from a plain program's by a relative error of at most 0.0035.
Values may be sent and summed in bfloat16 or wider, within the bound.
No kernel may reach another device: no remote copies, remote signals or barrier semaphores. Data moves between devices by JAX's collectives and lax.ppermute only.
A program may use at most 64 MiB of HBM per device.

v0:
```python
import jax
import jax.numpy as jnp
from jax import lax
from jax.sharding import PartitionSpec as P

FIELDS = 8
BAG = 4
R_DEV = 256


def pair_list(fields):
    return [(i, j) for i in range(fields) for j in range(i + 1, fields)]


def on_device(pooled, cotangent, bilinear, bag_ids, bag_lens, row_home):
    pair_order = pair_list(FIELDS)
    samples = pooled.shape[0]
    width = pooled.shape[2]
    projected = jnp.einsum(
        "bfd,fde->bfe", pooled[:, : FIELDS - 1], bilinear, preferred_element_type=jnp.float32
    )
    upper_terms = []
    for i in range(FIELDS - 1):
        running = jnp.zeros((samples, width), jnp.float32)
        for p, (a, c) in enumerate(pair_order):
            if a == i:
                running = running + cotangent[:, p].astype(jnp.float32) * pooled[:, c].astype(
                    jnp.float32
                )
        upper_terms.append(running)
    upper_bf = jnp.stack(upper_terms, 1).astype(jnp.bfloat16)
    local_weight = jnp.einsum(
        "bfd,bfe->fde", pooled[:, : FIELDS - 1], upper_bf, preferred_element_type=jnp.float32
    )
    weight_grad = lax.psum(local_weight, ("gx", "gy"))
    back_terms = jnp.einsum("bfe,fde->bfd", upper_bf, bilinear, preferred_element_type=jnp.float32)
    field_list = []
    for i in range(FIELDS):
        running = back_terms[:, i] if i < FIELDS - 1 else jnp.zeros((samples, width), jnp.float32)
        for p, (a, c) in enumerate(pair_order):
            if c == i:
                running = running + cotangent[:, p].astype(jnp.float32) * projected[:, a]
        field_list.append(running)
    field_grads = jnp.stack(field_list, 1).astype(jnp.bfloat16)
    size_gx = lax.axis_size("gx")
    size_gy = lax.axis_size("gy")
    owners_all = size_gx * size_gy
    entries = samples * FIELDS * BAG
    capacity = max(1, 2 * entries // owners_all)
    sentinel = R_DEV * FIELDS
    field_index = jnp.arange(FIELDS, dtype=jnp.int32)[None, :, None]
    stored = row_home[field_index, bag_ids]
    live = jnp.arange(BAG, dtype=jnp.int32)[None, None, :] < bag_lens[:, :, None]
    owner = (stored // R_DEV).reshape(-1)
    target = jnp.where(live, stored % R_DEV * FIELDS + field_index, sentinel).reshape(-1)
    values = jnp.where(live[:, :, :, None], field_grads[:, :, None, :], jnp.zeros((), jnp.bfloat16))
    values = values.reshape(entries, width)
    block_rows = 128
    blocks = entries // block_rows
    owner_ids = jnp.arange(owners_all, dtype=jnp.int32)
    owner_table = (owner.reshape(blocks, block_rows, 1) == owner_ids[None, None, :]).astype(
        jnp.bfloat16
    )
    row_pos = jnp.arange(block_rows, dtype=jnp.int32)
    earlier = (row_pos[:, None] > row_pos[None, :]).astype(jnp.bfloat16)
    within_all = jnp.einsum("ij,bjo->bio", earlier, owner_table, preferred_element_type=jnp.float32)
    block_totals = jnp.sum(owner_table.astype(jnp.float32), axis=1)
    block_start = jnp.cumsum(block_totals, axis=0) - block_totals
    ahead = within_all + block_start[:, None, :]
    rank = jnp.sum(ahead * owner_table.astype(jnp.float32), axis=2).reshape(-1).astype(jnp.int32)
    place = owner * capacity + rank
    send_values = (
        jnp.zeros((owners_all * capacity, width), jnp.bfloat16)
        .at[place]
        .set(values, unique_indices=True)
    )
    send_target = (
        jnp.full((owners_all * capacity,), sentinel, jnp.int32)
        .at[place]
        .set(target, unique_indices=True)
    )
    send_values = send_values.reshape(size_gx, size_gy, capacity, width)
    send_target = send_target.reshape(size_gx, size_gy, capacity)
    got_values, got_target = (
        lax.all_to_all(
            lax.all_to_all(send_values, "gy", split_axis=1, concat_axis=1, tiled=True),
            "gx",
            split_axis=0,
            concat_axis=0,
            tiled=True,
        ),
        lax.all_to_all(
            lax.all_to_all(send_target, "gy", split_axis=1, concat_axis=1, tiled=True),
            "gx",
            split_axis=0,
            concat_axis=0,
            tiled=True,
        ),
    )
    summed = jax.ops.segment_sum(
        got_values.reshape(-1, width).astype(jnp.float32),
        got_target.reshape(-1),
        num_segments=sentinel + 1,
    )
    table_grad = summed[:sentinel].reshape(R_DEV, FIELDS, width)
    return (weight_grad, table_grad)


def solution(mesh):
    placed = (
        P(("gx", "gy"), None, None),
        P(("gx", "gy"), None, None),
        P(),
        P(("gx", "gy"), None, None),
        P(("gx", "gy"), None),
        P(),
    )
    return jax.shard_map(
        on_device,
        mesh=mesh,
        in_specs=placed,
        out_specs=(P(), P(("gx", "gy"), None, None)),
        check_vma=False,
    )
```

profile of v0, /device:TPU:0, one launch (start us, length us, event | category | flops | bytes accessed | tf_op | source)
XLA Modules:
  0.0 339.2 jit_solution(13678758075913814048)
XLA Ops:
  7.2 0.8 fusion.102
  8.5 25.5 %gather_fusion = s32[4096]{0:T(1024)S(1)} fusion(s32[8,8192]{1,0:T(8,128)S(1)} %copy-done, s32[4096]{0:T(1024)S(1)} %reshape.231), kind=kCustom, calls=%fused_computation | custom fusion | bytes 65536 | tf_op jit(solution)/shard_map/gather | solution.py:52
  34.9 0.3 lt.51
  35.7 15.5 %scatter_custom_fusion = s32[8192]{0:T(1024)S(1)} fusion(s32[4096]{0:T(1024)S(1)} %bitcast.64, s32[4096]{0:T(1024)S(1)} %fusion.98, s32[]{:T(128)} %constant.25.clone.1), kind=kCustom, calls=%fused_computation.188 | custom fusion | bytes 32772 | tf_op jit(solution)/shard_map/scatter | solution.py:80
  51.3 0.6 copy.221
  51.9 4.3 %all-to-all-start = ((s32[8,4,256]{2,0,1:T(8,128)}), s32[8,4,256]{2,0,1:T(8,128)S(1)}, u32[]{:S(2)}, u32[]{:S(2)}) async-start(s32[8,4,256]{2,0,1:T(8,128)} %copy.221), calls=%async_computation | async-start | bytes 65536 | tf_op jit(solution)/shard_map/all_to_all | solution.py:93
  56.3 0.4 fusion.109
  61.7 0.4 copy-done.3
  62.2 0.3 convolution_bitcast_fusion.1
  63.1 0.4 broadcast_in_dim.61
  63.4 13.8 %scatter_custom_fusion.1 = bf16[8192,128]{1,0:T(8,128)(2,1)S(1)} fusion(s32[4096]{0:T(1024)S(1)} %bitcast.65, bf16[4096,128]{1,0:T(8,128)(2,1)S(1)} %bitcast.58, bf16[]{:T(256)} %constant.49.clone.1, pred[4096]{0:T(1024)(128)(4,1)S(1)} %lt.51), kind=kCustom, calls=%fused_computation.14 | custom fusion | flops 524288 | bytes 3150848 | tf_op jit(solution)/shard_map/scatter | solution.py:75
  77.2 1.5 copy.227
  78.7 3.6 %all-to-all-start.2 = ((bf16[8,4,256,128]{3,2,0,1:T(8,128)(2,1)}), bf16[8,4,256,128]{3,2,0,1:T(8,128)(2,1)S(1)}, u32[]{:S(2)}, u32[]{:S(2)}) async-start(bf16[8,4,256,128]{3,2,0,1:T(8,128)(2,1)} %copy.227), calls=%async_computation.2 | async-start | bytes 4194304 | tf_op jit(solution)/shard_map/all_to_all | solution.py:86
  82.3 0.6 copy.222
  82.9 25.0 %all-to-all-done.2 = bf16[8,4,256,128]{3,2,0,1:T(8,128)(2,1)S(1)} async-done(((bf16[8,4,256,128]{3,2,0,1:T(8,128)(2,1)}), bf16[8,4,256,128]{3,2,0,1:T(8,128)(2,1)S(1)}, u32[]{:S(2)}, u32[]{:S(2)}) %all-to-all-start.2) | async-done | bytes 2097184 | tf_op jit(solution)/shard_map/all_to_all | solution.py:86
  107.9 6.3 %all-to-all-start.1 = ((s32[8,4,256]{2,1,0:T(4,128)}), s32[8,4,256]{2,1,0:T(4,128)S(1)}, u32[]{:S(2)}, u32[]{:S(2)}) async-start(s32[8,4,256]{2,1,0:T(4,128)} %copy.222), calls=%async_computation.1 | async-start | bytes 65536 | tf_op jit(solution)/shard_map/all_to_all | solution.py:92
  114.2 1.5 copy.228
  115.7 5.2 %all-to-all-done.1 = s32[8,4,256]{2,1,0:T(4,128)S(1)} async-done(((s32[8,4,256]{2,1,0:T(4,128)}), s32[8,4,256]{2,1,0:T(4,128)S(1)}, u32[]{:S(2)}, u32[]{:S(2)}) %all-to-all-start.1) | async-done | bytes 32800 | tf_op jit(solution)/shard_map/all_to_all | solution.py:92
  120.9 3.6 %all-to-all-start.3 = ((bf16[8,4,256,128]{3,2,1,0:T(8,128)(2,1)}), bf16[8,4,256,128]{3,2,1,0:T(8,128)(2,1)S(1)}, u32[]{:S(2)}, u32[]{:S(2)}) async-start(bf16[8,4,256,128]{3,2,1,0:T(8,128)(2,1)} %copy.228), calls=%async_computation.3 | async-start | bytes 4194304 | tf_op jit(solution)/shard_map/all_to_all | solution.py:85
  124.8 1.0 convolution_bitcast_fusion.2
  125.8 147.7 %all-reduce.2.cloned.1.call-done = f32[7,128,128]{1,2,0:T(8,128)} async-done(((f32[7,128,128]{1,2,0:T(8,128)}), f32[7,128,128]{1,2,0:T(8,128)}) %all-reduce.2.cloned.1.call-update) | async-done | bytes 458768 | tf_op jit(solution)/shard_map/psum | solution.py:35
  273.5 2.0 copy.229
  275.5 55.8 %scatter_custom_fusion.2 = f32[2049,128]{1,0:T(8,128)S(1)} fusion(s32[8192]{0:T(1024)S(1)} %bitcast.63, bf16[8192,128]{1,0:T(8,128)(2,1)S(1)} %bitcast.56, f32[]{:T(128)} %constant.21.clone.1), kind=kCustom, calls=%fused_computation.4 | custom fusion | flops 2097152 | bytes 3146244 | tf_op jit(solution)/shard_map/scatter-add | solution.py:100
  331.3 1.0 slice_bitcast_fusion
  (89 shorter events, 7.6 us)
Async XLA Ops:
  7.2 1.3 copy-start
  8.5 26.1 %copy-start.7 = (s32[128,8]{0,1:T(8,128)S(1)}, s32[128,8]{0,1:T(8,128)}, u32[]{:S(2)}) copy-start(s32[128,8]{0,1:T(8,128)} %param.10) | copy-start | bytes 12292
  34.0 22.2 %copy-start.6 = (bf16[128,28,128]{2,0,1:T(8,128)(2,1)S(1)}, bf16[128,28,128]{2,0,1:T(8,128)(2,1)}, u32[]{:S(2)}) copy-start(bf16[128,28,128]{2,0,1:T(8,128)(2,1)} %param.7) | copy-start | bytes 2752516
  34.3 22.0 %copy-start.1 = (bf16[128,8,128]{2,1,0:T(8,128)(2,1)S(1)}, bf16[128,8,128]{2,1,0:T(8,128)(2,1)}, u32[]{:S(2)}) copy-start(bf16[128,8,128]{2,1,0:T(8,128)(2,1)} %param.6) | copy-start | bytes 786436
  51.9 26.8 %all-to-all-start = ((s32[8,4,256]{2,0,1:T(8,128)}), s32[8,4,256]{2,0,1:T(8,128)S(1)}, u32[]{:S(2)}, u32[]{:S(2)}) async-start(s32[8,4,256]{2,0,1:T(8,128)} %copy.221), calls=%async_computation | async-start | bytes 65536 | tf_op jit(solution)/shard_map/all_to_all | solution.py:93
  57.3 4.2 %copy-start.5 = (bf16[7,128,128]{2,1,0:T(8,128)(2,1)S(1)}, bf16[7,128,128]{2,1,0:T(8,128)(2,1)}, u32[]{:S(2)}) copy-start(bf16[7,128,128]{2,1,0:T(8,128)(2,1)} %param.8) | copy-start | bytes 688132
  61.5 0.7 copy-start.3
  78.7 29.2 %all-to-all-start.2 = ((bf16[8,4,256,128]{3,2,0,1:T(8,128)(2,1)}), bf16[8,4,256,128]{3,2,0,1:T(8,128)(2,1)S(1)}, u32[]{:S(2)}, u32[]{:S(2)}) async-start(bf16[8,4,256,128]{3,2,0,1:T(8,128)(2,1)} %copy.227), calls=%async_computation.2 | async-start | bytes 4194304 | tf_op jit(solution)/shard_map/all_to_all | solution.py:86
  107.9 13.0 %all-to-all-start.1 = ((s32[8,4,256]{2,1,0:T(4,128)}), s32[8,4,256]{2,1,0:T(4,128)S(1)}, u32[]{:S(2)}, u32[]{:S(2)}) async-start(s32[8,4,256]{2,1,0:T(4,128)} %copy.222), calls=%async_computation.1 | async-start | bytes 65536 | tf_op jit(solution)/shard_map/all_to_all | solution.py:92
  115.7 9.1 %copy-start.2 = (bf16[128,8,128]{2,1,0:T(8,128)(2,1)S(1)}, bf16[128,8,128]{2,1,0:T(8,128)(2,1)}, u32[]{:S(2)}) copy-start(bf16[128,8,128]{2,1,0:T(8,128)(2,1)} %param.6) | copy-start | bytes 786436
  115.7 9.1 %copy-start.4 = (bf16[128,7,128]{0,2,1:T(8,128)(2,1)S(1)}, bf16[128,7,128]{0,2,1:T(8,128)(2,1)}, u32[]{:S(2)}) copy-start(bf16[128,7,128]{0,2,1:T(8,128)(2,1)} %copy-done.3) | copy-start | bytes 688132
  120.9 154.6 %all-to-all-start.3 = ((bf16[8,4,256,128]{3,2,1,0:T(8,128)(2,1)}), bf16[8,4,256,128]{3,2,1,0:T(8,128)(2,1)S(1)}, u32[]{:S(2)}, u32[]{:S(2)}) async-start(bf16[8,4,256,128]{3,2,1,0:T(8,128)(2,1)} %copy.228), calls=%async_computation.3 | async-start | bytes 4194304 | tf_op jit(solution)/shard_map/all_to_all | solution.py:85
  124.5 149.0 %all-reduce.2.cloned.1.call-start = ((), (), s32[]{:S(2)}) async-start(), calls=%async_computation.4 | async-start | bytes 917504 | tf_op jit(solution)/shard_map/psum | solution.py:35
Sparse Core Ops, SparseCore 0:
  131.2 142.2 all-reduce.1
where the time goes:
time: 340 us; the launch traced here: 339 us
  waiting for transfers between devices  178 us (52%)
  other arithmetic  71.7 us (21%)
  local copies, waits for them, and re-layouts  55.3 us (16%)
  starting transfers between devices  18 us (5%)
  between operations  14.5 us (4%)
    psum x1, waiting for transfers between devices, on_device(): weight_grad = lax.psum(local_weight, ('gx', 'gy'))  148 us
    scatter-add x1, other arithmetic, on_device(): jax.ops.segment_sum(got_values.reshape(-1, width).astype(jnp.float32), go...  55.8 us
    gather x1, local copies, waits for them, and re-layouts, on_device(): stored = row_home[field_index, bag_ids]  25.5 us
    all_to_all x1, waiting for transfers between devices, on_device(): lax.all_to_all(send_values, 'gy', split_axis=1, concat_axis=1, tiled=True)  25 us
    scatter x1, local copies, waits for them, and re-layouts, on_device(): send_target = jnp.full((owners_all * capacity,), sentinel, jnp.int32).at[...  15.5 us
    scatter x1, other arithmetic, on_device(): send_values = jnp.zeros((owners_all * capacity, width), jnp.bfloat16).at[...  13.8 us
    unnamed x55, local copies, waits for them, and re-layouts  6.81 us
  transfers between devices with their start and end apart: 5, of which 3 were waited for; matrix products, arithmetic and copies ran while one was open for 8% of the time, Pallas kernels for 0%

commit v1 on v0

--- a/solution.py
+++ b/solution.py
@@ -32,7 +32,7 @@
     local_weight = jnp.einsum(
         "bfd,bfe->fde", pooled[:, : FIELDS - 1], upper_bf, preferred_element_type=jnp.float32
     )
-    weight_grad = lax.psum(local_weight, ("gx", "gy"))
+    weight_grad = jnp.sum(lax.all_gather(local_weight, ("gx", "gy")), axis=0)
     back_terms = jnp.einsum("bfe,fde->bfd", upper_bf, bilinear, preferred_element_type=jnp.float32)
     field_list = []
     for i in range(FIELDS):

time: 340 us -> 262 us (0.77)
  waiting for transfers between devices: 178 us -> 94 us
  other arithmetic: 71.7 us -> 77.8 us
    psum x1 -> x0, waiting for transfers between devices: 148 us -> none  [on_device(): weight_grad = lax.psum(local_weight, ('gx', 'gy'))]
    all_to_all x1, waiting for transfers between devices: 0.01 us -> 47.3 us  [on_device(): lax.all_to_all(lax.all_to_all(send_values, 'gy', split_axis=1, concat_axi...]
    all_to_all x1, waiting for transfers between devices: 25 us -> 41.4 us  [on_device(): lax.all_to_all(send_values, 'gy', split_axis=1, concat_axis=1, tiled=True)]
    reduce_sum x0 -> x1, other arithmetic: none -> 6.83 us  [on_device(): weight_grad = jnp.sum(lax.all_gather(local_weight, ('gx', 'gy')), axis=0)]
    unnamed x55 -> x166, local copies, waits for them, and re-layouts: 6.81 us -> 5.24 us
  transfers between devices with their start and end apart: 5 -> 5, of which waited for: 3 -> 3; matrix products, arithmetic and copies ran while one was open for 8% -> 46% of each run, Pallas kernels for 0% -> 0%
where the time goes in v1:
time: 262 us
  waiting for transfers between devices  94 us (36%)
  other arithmetic  77.8 us (30%)
  local copies, waits for them, and re-layouts  56.6 us (22%)
  starting transfers between devices  17.2 us (7%)
  between operations  15.3 us (6%)
    scatter-add x1, other arithmetic, on_device(): jax.ops.segment_sum(got_values.reshape(-1, width).astype(jnp.float32), go...  55.8 us
    all_to_all x1, waiting for transfers between devices, on_device(): lax.all_to_all(lax.all_to_all(send_values, 'gy', split_axis=1, concat_axi...  47.3 us
    all_to_all x1, waiting for transfers between devices, on_device(): lax.all_to_all(send_values, 'gy', split_axis=1, concat_axis=1, tiled=True)  41.4 us
    gather x1, local copies, waits for them, and re-layouts, on_device(): stored = row_home[field_index, bag_ids]  25.5 us
    scatter x1, local copies, waits for them, and re-layouts, on_device(): send_target = jnp.full((owners_all * capacity,), sentinel, jnp.int32).at[...  15.5 us
    scatter x1, other arithmetic, on_device(): send_values = jnp.zeros((owners_all * capacity, width), jnp.bfloat16).at[...  13.8 us
    reduce_sum x1, other arithmetic, on_device(): weight_grad = jnp.sum(lax.all_gather(local_weight, ('gx', 'gy')), axis=0)  6.83 us
    all_to_all x1, starting transfers between devices, on_device(): lax.all_to_all(lax.all_to_all(send_target, 'gy', split_axis=1, concat_axi...  5.51 us
  transfers between devices with their start and end apart: 5, of which 3 were waited for; matrix products, arithmetic and copies ran while one was open for 46% of the time, Pallas kernels for 0%

profile of v1, /device:TPU:0, one launch (start us, length us, event | category | flops | bytes accessed | tf_op | source)
XLA Modules:
  0.0 261.9 jit_solution(16736044657954954828)
XLA Ops:
  7.2 1.0 fusion.108
  8.2 1.1 fusion.107
  9.3 0.4 fusion.109
  14.8 0.7 copy-done.3
  15.8 1.0 copy.221
  17.4 25.5 %gather_fusion = s32[4096]{0:T(1024)S(1)} fusion(s32[8,8192]{1,0:T(8,128)S(1)} %copy-done, s32[4096]{0:T(1024)S(1)} %reshape.231), kind=kCustom, calls=%fused_computation | custom fusion | bytes 65536 | tf_op jit(solution)/shard_map/gather | solution.py:52
  43.9 0.3 lt.51
  44.9 15.5 %scatter_custom_fusion = s32[8192]{0:T(1024)S(1)} fusion(s32[4096]{0:T(1024)S(1)} %bitcast.66, s32[4096]{0:T(1024)S(1)} %fusion.98, s32[]{:T(128)} %constant.25.clone.1), kind=kCustom, calls=%fused_computation.188 | custom fusion | bytes 32772 | tf_op jit(solution)/shard_map/scatter | solution.py:80
  60.4 0.6 copy.225
  61.1 4.3 %all-to-all-start = ((s32[8,4,256]{2,0,1:T(8,128)}), s32[8,4,256]{2,0,1:T(8,128)S(1)}, u32[]{:S(2)}, u32[]{:S(2)}) async-start(s32[8,4,256]{2,0,1:T(8,128)} %copy.225), calls=%async_computation | async-start | bytes 65536 | tf_op jit(solution)/shard_map/all_to_all | solution.py:93
  66.8 0.4 broadcast_in_dim.61
  67.2 13.8 %scatter_custom_fusion.1 = bf16[8192,128]{1,0:T(8,128)(2,1)S(1)} fusion(s32[4096]{0:T(1024)S(1)} %bitcast.67, bf16[4096,128]{1,0:T(8,128)(2,1)S(1)} %bitcast.60, bf16[]{:T(256)} %constant.49.clone.1, pred[4096]{0:T(1024)(128)(4,1)S(1)} %lt.51), kind=kCustom, calls=%fused_computation.14 | custom fusion | flops 524288 | bytes 3150848 | tf_op jit(solution)/shard_map/scatter | solution.py:75
  80.9 1.4 copy.231
  82.4 3.6 %all-to-all-start.2 = ((bf16[8,4,256,128]{3,2,0,1:T(8,128)(2,1)}), bf16[8,4,256,128]{3,2,0,1:T(8,128)(2,1)S(1)}, u32[]{:S(2)}, u32[]{:S(2)}) async-start(bf16[8,4,256,128]{3,2,0,1:T(8,128)(2,1)} %copy.231), calls=%async_computation.2 | async-start | bytes 4194304 | tf_op jit(solution)/shard_map/all_to_all | solution.py:86
  86.0 0.6 copy.226
  86.6 41.4 %all-to-all-done.2 = bf16[8,4,256,128]{3,2,0,1:T(8,128)(2,1)S(1)} async-done(((bf16[8,4,256,128]{3,2,0,1:T(8,128)(2,1)}), bf16[8,4,256,128]{3,2,0,1:T(8,128)(2,1)S(1)}, u32[]{:S(2)}, u32[]{:S(2)}) %all-to-all-start.2) | async-done | bytes 2097184 | tf_op jit(solution)/shard_map/all_to_all | solution.py:86
  128.0 5.5 %all-to-all-start.1 = ((s32[8,4,256]{2,1,0:T(4,128)}), s32[8,4,256]{2,1,0:T(4,128)S(1)}, u32[]{:S(2)}, u32[]{:S(2)}) async-start(s32[8,4,256]{2,1,0:T(4,128)} %copy.226), calls=%async_computation.1 | async-start | bytes 65536 | tf_op jit(solution)/shard_map/all_to_all | solution.py:92
  133.5 1.4 copy.232
  135.0 5.2 %all-to-all-done.1 = s32[8,4,256]{2,1,0:T(4,128)S(1)} async-done(((s32[8,4,256]{2,1,0:T(4,128)}), s32[8,4,256]{2,1,0:T(4,128)S(1)}, u32[]{:S(2)}, u32[]{:S(2)}) %all-to-all-start.1) | async-done | bytes 32800 | tf_op jit(solution)/shard_map/all_to_all | solution.py:92
  140.2 3.8 %all-to-all-start.3 = ((bf16[8,4,256,128]{3,2,1,0:T(8,128)(2,1)}), bf16[8,4,256,128]{3,2,1,0:T(8,128)(2,1)S(1)}, u32[]{:S(2)}, u32[]{:S(2)}) async-start(bf16[8,4,256,128]{3,2,1,0:T(8,128)(2,1)} %copy.232), calls=%async_computation.3 | async-start | bytes 4194304 | tf_op jit(solution)/shard_map/all_to_all | solution.py:85
  144.0 47.3 %all-to-all-done.3 = bf16[8,4,256,128]{3,2,1,0:T(8,128)(2,1)S(1)} async-done(((bf16[8,4,256,128]{3,2,1,0:T(8,128)(2,1)}), bf16[8,4,256,128]{3,2,1,0:T(8,128)(2,1)S(1)}, u32[]{:S(2)}, u32[]{:S(2)}) %all-to-all-start.3) | async-done | bytes 2097184 | tf_op jit(solution)/shard_map/all_to_all | solution.py:85
  191.4 55.8 %scatter_custom_fusion.2 = f32[2049,128]{1,0:T(8,128)S(1)} fusion(s32[8192]{0:T(1024)S(1)} %bitcast.65, bf16[8192,128]{1,0:T(8,128)(2,1)S(1)} %bitcast.58, f32[]{:T(128)} %constant.21.clone.1), kind=kCustom, calls=%fused_computation.4 | custom fusion | flops 2097152 | bytes 3146244 | tf_op jit(solution)/shard_map/scatter-add | solution.py:100
  247.2 1.0 slice_bitcast_fusion
  248.2 6.8 %reduce_sum.27 = f32[7,128,128]{2,1,0:T(8,128)} reduce(f32[32,7,128,128]{3,2,1,0:T(8,128)} %bitcast.57, f32[]{:T(128)} %constant.21.clone.1), dimensions={0}, to_apply=%region_0.0 | reduce | flops 3555328 | bytes 15138820 | tf_op jit(solution)/shard_map/reduce_sum | solution.py:35
  (202 shorter events, 8.0 us)
Async XLA Ops:
  7.2 241.0 %all-gather.3.cloned.1.call-start = ((), (), s32[]{:S(2)}) async-start(), calls=%async_computation.4 | async-start | bytes 15138816 | tf_op jit(solution)/shard_map/all_gather | solution.py:35
  17.4 26.2 %copy-start.63 = (s32[128,8]{0,1:T(8,128)S(1)}, s32[128,8]{0,1:T(8,128)}, u32[]{:S(2)}) copy-start(s32[128,8]{0,1:T(8,128)} %param.10) | copy-start | bytes 12292
  42.9 22.4 %copy-start.4 = (bf16[128,7,128]{0,2,1:T(8,128)(2,1)S(1)}, bf16[128,7,128]{0,2,1:T(8,128)(2,1)}, u32[]{:S(2)}) copy-start(bf16[128,7,128]{0,2,1:T(8,128)(2,1)} %copy-done.3) | copy-start | bytes 688132
  42.9 22.4 %copy-start.5 = (bf16[7,128,128]{2,1,0:T(8,128)(2,1)S(1)}, bf16[7,128,128]{2,1,0:T(8,128)(2,1)}, u32[]{:S(2)}) copy-start(bf16[7,128,128]{2,1,0:T(8,128)(2,1)} %param.8) | copy-start | bytes 688132
  42.9 22.7 %copy-start.2 = (bf16[128,8,128]{2,1,0:T(8,128)(2,1)S(1)}, bf16[128,8,128]{2,1,0:T(8,128)(2,1)}, u32[]{:S(2)}) copy-start(bf16[128,8,128]{2,1,0:T(8,128)(2,1)} %param.6) | copy-start | bytes 786436
  43.3 22.7 %copy-start.49 = (bf16[128,1,128]{0,2,1:T(8,128)(2,1)S(1)}, bf16[128,1,128]{0,2,1:T(8,128)(2,1)}, u32[]{:S(2)}) copy-start(bf16[128,1,128]{0,2,1:T(8,128)(2,1)} %copy-done.48) | copy-start | bytes 98308
  43.5 22.4 %copy-start.29 = (bf16[128,1,128]{0,2,1:T(8,128)(2,1)S(1)}, bf16[128,1,128]{0,2,1:T(8,128)(2,1)}, u32[]{:S(2)}) copy-start(bf16[128,1,128]{0,2,1:T(8,128)(2,1)} %copy-done.28) | copy-start | bytes 98308
  43.6 22.4 %copy-start.39 = (bf16[128,1,128]{0,2,1:T(8,128)(2,1)S(1)}, bf16[128,1,128]{0,2,1:T(8,128)(2,1)}, u32[]{:S(2)}) copy-start(bf16[128,1,128]{0,2,1:T(8,128)(2,1)} %copy-done.38) | copy-start | bytes 98308
  43.6 22.4 %copy-start.27 = (bf16[128,1,128]{0,2,1:T(8,128)(2,1)S(1)}, bf16[128,1,128]{0,2,1:T(8,128)(2,1)}, u32[]{:S(2)}) copy-start(bf16[128,1,128]{0,2,1:T(8,128)(2,1)} %copy-done.26) | copy-start | bytes 98308
  43.6 22.4 %copy-start.31 = (bf16[128,1,128]{0,2,1:T(8,128)(2,1)S(1)}, bf16[128,1,128]{0,2,1:T(8,128)(2,1)}, u32[]{:S(2)}) copy-start(bf16[128,1,128]{0,2,1:T(8,128)(2,1)} %copy-done.30) | copy-start | bytes 98308
  43.6 22.4 %copy-start.37 = (bf16[128,1,128]{0,2,1:T(8,128)(2,1)S(1)}, bf16[128,1,128]{0,2,1:T(8,128)(2,1)}, u32[]{:S(2)}) copy-start(bf16[128,1,128]{0,2,1:T(8,128)(2,1)} %copy-done.36) | copy-start | bytes 98308
  44.3 21.8 %copy-start.47 = (bf16[128,1,128]{0,2,1:T(8,128)(2,1)S(1)}, bf16[128,1,128]{0,2,1:T(8,128)(2,1)}, u32[]{:S(2)}) copy-start(bf16[128,1,128]{0,2,1:T(8,128)(2,1)} %copy-done.46) | copy-start | bytes 98308
  44.3 21.8 %copy-start.53 = (bf16[128,1,128]{0,2,1:T(8,128)(2,1)S(1)}, bf16[128,1,128]{0,2,1:T(8,128)(2,1)}, u32[]{:S(2)}) copy-start(bf16[128,1,128]{0,2,1:T(8,128)(2,1)} %copy-done.52) | copy-start | bytes 98308
  44.3 21.8 %copy-start.57 = (bf16[128,1,128]{0,2,1:T(8,128)(2,1)S(1)}, bf16[128,1,128]{0,2,1:T(8,128)(2,1)}, u32[]{:S(2)}) copy-start(bf16[128,1,128]{0,2,1:T(8,128)(2,1)} %copy-done.56) | copy-start | bytes 98308
  44.3 21.8 %copy-start.61 = (bf16[128,1,128]{0,2,1:T(8,128)(2,1)S(1)}, bf16[128,1,128]{0,2,1:T(8,128)(2,1)}, u32[]{:S(2)}) copy-start(bf16[128,1,128]{0,2,1:T(8,128)(2,1)} %copy-done.60) | copy-start | bytes 98308
  44.3 21.8 %copy-start.15 = (bf16[128,1,128]{0,2,1:T(8,128)(2,1)S(1)}, bf16[128,1,128]{0,2,1:T(8,128)(2,1)}, u32[]{:S(2)}) copy-start(bf16[128,1,128]{0,2,1:T(8,128)(2,1)} %copy-done.14) | copy-start | bytes 98308
  44.4 21.8 %copy-start.17 = (bf16[128,1,128]{0,2,1:T(8,128)(2,1)S(1)}, bf16[128,1,128]{0,2,1:T(8,128)(2,1)}, u32[]{:S(2)}) copy-start(bf16[128,1,128]{0,2,1:T(8,128)(2,1)} %copy-done.16) | copy-start | bytes 98308
  44.4 21.8 %copy-start.21 = (bf16[128,1,128]{0,2,1:T(8,128)(2,1)S(1)}, bf16[128,1,128]{0,2,1:T(8,128)(2,1)}, u32[]{:S(2)}) copy-start(bf16[128,1,128]{0,2,1:T(8,128)(2,1)} %copy-done.20) | copy-start | bytes 98308
  44.4 21.8 %copy-start.25 = (bf16[128,1,128]{0,2,1:T(8,128)(2,1)S(1)}, bf16[128,1,128]{0,2,1:T(8,128)(2,1)}, u32[]{:S(2)}) copy-start(bf16[128,1,128]{0,2,1:T(8,128)(2,1)} %copy-done.24) | copy-start | bytes 98308
  44.4 21.8 %copy-start.35 = (bf16[128,1,128]{0,2,1:T(8,128)(2,1)S(1)}, bf16[128,1,128]{0,2,1:T(8,128)(2,1)}, u32[]{:S(2)}) copy-start(bf16[128,1,128]{0,2,1:T(8,128)(2,1)} %copy-done.34) | copy-start | bytes 98308
  61.1 21.3 %all-to-all-start = ((s32[8,4,256]{2,0,1:T(8,128)}), s32[8,4,256]{2,0,1:T(8,128)S(1)}, u32[]{:S(2)}, u32[]{:S(2)}) async-start(s32[8,4,256]{2,0,1:T(8,128)} %copy.225), calls=%async_computation | async-start | bytes 65536 | tf_op jit(solution)/shard_map/all_to_all | solution.py:93
  82.4 45.7 %all-to-all-start.2 = ((bf16[8,4,256,128]{3,2,0,1:T(8,128)(2,1)}), bf16[8,4,256,128]{3,2,0,1:T(8,128)(2,1)S(1)}, u32[]{:S(2)}, u32[]{:S(2)}) async-start(bf16[8,4,256,128]{3,2,0,1:T(8,128)(2,1)} %copy.231), calls=%async_computation.2 | async-start | bytes 4194304 | tf_op jit(solution)/shard_map/all_to_all | solution.py:86
  128.0 12.2 %all-to-all-start.1 = ((s32[8,4,256]{2,1,0:T(4,128)}), s32[8,4,256]{2,1,0:T(4,128)S(1)}, u32[]{:S(2)}, u32[]{:S(2)}) async-start(s32[8,4,256]{2,1,0:T(4,128)} %copy.226), calls=%async_computation.1 | async-start | bytes 65536 | tf_op jit(solution)/shard_map/all_to_all | solution.py:92
  140.2 51.2 %all-to-all-start.3 = ((bf16[8,4,256,128]{3,2,1,0:T(8,128)(2,1)}), bf16[8,4,256,128]{3,2,1,0:T(8,128)(2,1)S(1)}, u32[]{:S(2)}, u32[]{:S(2)}) async-start(bf16[8,4,256,128]{3,2,1,0:T(8,128)(2,1)} %copy.232), calls=%async_computation.3 | async-start | bytes 4194304 | tf_op jit(solution)/shard_map/all_to_all | solution.py:85
  (45 other events, 248.5 us)
Sparse Core Ops, SparseCore 0:
  17.0 122.2 all-gather.2
